TPU v7x, 8 devices: a whole 2x2x1 slice. The times are simulated.
8 devices in a mesh: ez: 2 (over z, y), ey: 2 (over x), ex: 2 (over core).
Axes of the slice: x: 2, y: 2, z: 1, core: 2. Of those that a mesh axis runs over, the one named last changes fastest.
Arguments:
- tokens: bfloat16 [2048, 2048], P(('ez', 'ey', 'ex'))
- expert_ids: int32 [2048, 6], P(('ez', 'ey', 'ex'))
- gate_weights: float32 [2048, 6], P(('ez', 'ey', 'ex'))
- w_gate: bfloat16 [64, 2048, 1408], P(('ez', 'ey', 'ex'))
- w_up: bfloat16 [64, 2048, 1408], P(('ez', 'ey', 'ex'))
- w_down: bfloat16 [64, 1408, 2048], P(('ez', 'ey', 'ex'))
Outputs:
- output: bfloat16 [2048, 2048], P(('ez', 'ey', 'ex'))
All inputs are finite; a program needn't handle non-finite values.
Results may differ from a plain program's by a relative error of at most 0.00619725.
Values are sent between devices in bfloat16 or wider.
A program may use at most 1 GiB of HBM per device.

v0:
```python
import math
import jax
import jax.numpy as jnp
from jax import lax
from jax.sharding import PartitionSpec as P


def pack_rows(chosen, gate_vals, per_expert):
    row_rank = jnp.cumsum(chosen.astype(jnp.int32), axis=0) - 1
    slot_idx = jnp.where(chosen, row_rank, per_expert)
    row_idx = jnp.broadcast_to(jnp.arange(chosen.shape[0])[:, None], chosen.shape)
    exp_idx = jnp.broadcast_to(jnp.arange(chosen.shape[1])[None, :], chosen.shape)
    pick_rows = jnp.zeros((chosen.shape[1], per_expert), jnp.int32).at[exp_idx, slot_idx].set(row_idx, mode="drop")
    pick_gates = jnp.zeros((chosen.shape[1], per_expert), jnp.float32).at[exp_idx, slot_idx].set(gate_vals, mode="drop")
    return pick_rows, pick_gates


def expert_ffn(x_pack, w_gate, w_up, w_down, pick_gates):
    gate_act = jnp.einsum("lch,lhf->lcf", x_pack, w_gate, preferred_element_type=jnp.float32)
    up_act = jnp.einsum("lch,lhf->lcf", x_pack, w_up, preferred_element_type=jnp.float32)
    hidden_act = (jax.nn.silu(gate_act) * up_act).astype(jnp.bfloat16)
    expert_out = jnp.einsum("lcf,lfh->lch", hidden_act, w_down, preferred_element_type=jnp.float32)
    return expert_out * pick_gates[:, :, None]


def solution(mesh):
    ep_axes = tuple(mesh.axis_names)
    num_devices = math.prod(mesh.shape[axis_name] for axis_name in ep_axes)
    row_spec = P(ep_axes, None)
    w_spec = P(ep_axes, None, None)

    def local_layer(tokens, expert_ids, gate_weights, w_gate, w_up, w_down):
        tok_dev, hidden = tokens.shape
        top_k = expert_ids.shape[1]
        local_experts = w_gate.shape[0]
        capacity = tok_dev * top_k // num_devices
        rows_recv = num_devices * capacity
        per_expert = rows_recv // local_experts
        dest_dev = expert_ids // local_experts
        dev_hit = jnp.any(dest_dev[:, :, None] == jnp.arange(num_devices)[None, None, :], axis=1)
        all_experts = jnp.arange(num_devices * local_experts)
        gate_dense = jnp.sum(jnp.where(expert_ids[:, :, None] == all_experts[None, None, :], gate_weights[:, :, None], 0.0), axis=1)
        gate_dense = gate_dense.reshape(tok_dev, num_devices, local_experts)
        slot_pos = jnp.cumsum(dev_hit.astype(jnp.int32), axis=0) - 1
        place_mask = dev_hit[:, :, None] & (slot_pos[:, :, None] == jnp.arange(capacity)[None, None, :])
        place_bf = place_mask.astype(jnp.bfloat16)
        send_rows = jnp.einsum("tdc,th->dch", place_bf, tokens, preferred_element_type=jnp.float32).astype(jnp.bfloat16)
        send_gates = jnp.sum(jnp.where(place_mask[:, :, :, None], gate_dense[:, :, None, :], 0.0), axis=0)
        recv_rows = lax.all_to_all(send_rows, ep_axes, 0, 0, tiled=True)
        recv_gates = lax.all_to_all(send_gates, ep_axes, 0, 0, tiled=True)
        flat_rows = recv_rows.reshape(rows_recv, hidden)
        flat_gates = recv_gates.reshape(rows_recv, local_experts)
        pick_rows, pick_gates = pack_rows(flat_gates > 0.0, flat_gates, per_expert)
        weighted = expert_ffn(flat_rows[pick_rows], w_gate, w_up, w_down, pick_gates)
        part_sum = jax.ops.segment_sum(weighted.reshape(-1, hidden), pick_rows.reshape(-1), num_segments=rows_recv)
        back_rows = part_sum.astype(jnp.bfloat16).reshape(num_devices, capacity, hidden)
        returned = lax.all_to_all(back_rows, ep_axes, 0, 0, tiled=True)
        moe_sum = jnp.einsum("tdc,dch->th", place_bf, returned, preferred_element_type=jnp.float32)
        return (tokens.astype(jnp.float32) + moe_sum).astype(jnp.bfloat16)

    return jax.shard_map(local_layer, mesh=mesh, in_specs=(row_spec, row_spec, row_spec, w_spec, w_spec, w_spec), out_specs=row_spec, check_vma=False)
```

profile of v0, /device:TPU:0, one launch (start us, length us, event | category | flops | bytes accessed | tf_op | source)
XLA Modules:
  0.0 307.5 jit_solution(820671461984669227)
XLA Ops:
  0.0 0.7 add_select_fusion
  0.7 0.6 reduce-window.14
  1.3 0.2 slice_reduce_fusion.1
  1.6 0.1 add_bitcast_fusion.1
  1.7 0.8 select_reduce_fusion.1
  2.4 0.3 fusion.6
  2.7 1.9 select_reduce_fusion
  4.6 0.9 copy.27
  5.6 4.3 %all-to-all-start = ((f32[8,192,8]{1,2,0:T(8,128)}), f32[8,192,8]{1,2,0:T(8,128)S(1)}, u32[]{:S(2)}, u32[]{:S(2)}) async-start(f32[8,192,8]{1,2,0:T(8,128)} %copy.27), calls=%async_computation | async-start | bytes 131072 | tf_op jit(solution)/shard_map/all_to_all | solution.py:50
  9.9 5.7 %convolution_convert_fusion = bf16[8,192,2048]{2,1,0:T(8,128)(2,1)} fusion(bf16[256,2048]{1,0:T(8,128)(2,1)} %param.6, s32[256,8]{0,1:T(8,128)S(1)} %add_bitcast_fusion.1, pred[256,8]{0,1:T(8,128)(4,1)S(1)} %fusion.10), kind=kOutput, calls=%fused_computation.10 | convolution fusion | flops 1614544896 | bytes 7350272 | tf_op jit(solution)/shard_map/tdc,th->dch/dot_general | solution.py:47
  15.6 0.0 copy-start.2
  15.6 0.0 copy-start.1
  15.6 0.0 all-to-all-done
  15.6 3.6 %all-to-all-start.1 = ((bf16[8,192,2048]{2,1,0:T(8,128)(2,1)}), bf16[8,192,2048]{2,1,0:T(8,128)(2,1)}, u32[]{:S(2)}, u32[]{:S(2)}) async-start(bf16[8,192,2048]{2,1,0:T(8,128)(2,1)} %convolution_convert_fusion), calls=%async_computation.1 | async-start | bytes 12582912 | tf_op jit(solution)/shard_map/all_to_all | solution.py:49
  19.2 0.1 broadcast_in_dim.85
  19.2 0.4 reshape.96
  19.6 0.1 reshape.111
  19.8 2.3 reduce-window.16
  22.1 0.3 slice_reduce_fusion
  22.4 0.2 reduce-window.19
  22.5 0.3 copy.31
  22.8 0.4 reshape.102
  23.2 0.1 add_bitcast_fusion
  23.3 0.0 copy-done.2
  23.3 0.1 multiply_reduce_fusion
  23.4 0.0 copy-done.1
  23.4 0.1 and_reduce_fusion
  23.5 0.3 copy.30
  23.8 0.4 reshape.94
  24.1 45.4 %scatter_custom_fusion.2 = f32[1536]{0:T(1024)S(1)} fusion(s32[12288]{0:T(1024)S(1)} %reshape.94, f32[12288]{0:T(1024)S(1)} %reshape.102, f32[]{:T(128)} %constant.41.clone.1), kind=kCustom, calls=%fused_computation.46 | custom fusion | bytes 6148
  69.5 0.1 reshape.74
  69.6 45.6 %scatter_custom_fusion.1 = s32[1536]{0:T(1024)S(1)} fusion(s32[12288]{0:T(1024)S(1)} %reshape.94, s32[12288]{0:T(1024)S(1)} %reshape.96, s32[]{:T(128)} %constant.20.clone.1), kind=kCustom, calls=%fused_computation.48 | custom fusion | bytes 6148 | tf_op jit(solution)/shard_map/broadcast_in_dim;reshape | solution.py:55
  115.1 0.1 reshape.70
  115.2 0.1 reshape.80
  115.3 0.0 all-to-all-done.1
  115.3 16.3 %gather_fusion = bf16[1536,2048]{1,0:T(8,128)(2,1)} fusion(bf16[1536,2048]{1,0:T(8,128)(2,1)} %bitcast.10, s32[2048]{0:T(1024)S(1)} %pad_clamp_fusion), kind=kCustom, calls=%fused_computation | custom fusion | bytes 12589056 | tf_op jit(solution)/shard_map/gather | solution.py:54
  131.6 22.2 %fusion.20 = f32[8,192,1408]{2,1,0:T(8,128)} fusion(bf16[8,192,2048]{2,1,0:T(8,128)(2,1)} %bitcast.63, bf16[8,2048,1408]{2,1,0:T(8,128)(2,1)} %param.9), kind=kOutput, calls=%fused_computation.51 | convolution fusion | flops 8858370048 | bytes 61079552 | tf_op jit(solution)/shard_map/lch,lhf->lcf/dot_general | solution.py:19
  153.8 23.1 %multiply_convert_fusion.clone.6 = bf16[8,192,1408]{2,1,0:T(8,128)(2,1)S(1)} fusion(f32[8,192,1408]{2,1,0:T(8,128)} %fusion.20, bf16[8,192,2048]{2,1,0:T(8,128)(2,1)} %bitcast.64, bf16[8,2048,1408]{2,1,0:T(8,128)(2,1)} %param.10), kind=kOutput, calls=%fused_computation.5.clone.clone.clone.clone.clone.1 | convolution fusion | flops 8871346176 | bytes 65404928 | tf_op jit(solution)/shard_map/lch,lhf->lcf/dot_general | solution.py:20
  177.0 21.5 %broadcast_multiply_fusion = f32[8,192,2048]{2,1,0:T(8,128)} fusion(f32[8,192]{1,0:T(8,128)S(1)} %reshape.74, bf16[8,1408,2048]{2,1,0:T(8,128)(2,1)} %param.11, bf16[8,192,1408]{2,1,0:T(8,128)(2,1)S(1)} %multiply_convert_fusion.clone.6), kind=kOutput, calls=%fused_computation.6 | convolution fusion | flops 8861515776 | bytes 63051776 | tf_op jit(solution)/shard_map/lcf,lfh->lch/dot_general | solution.py:22
  198.5 26.4 %scatter_custom_fusion = f32[1536,2048]{1,0:T(8,128)} fusion(s32[1536]{0:T(1024)S(1)} %scatter_custom_fusion.1, f32[1536,2048]{1,0:T(8,128)} %bitcast.62, f32[]{:T(128)} %constant.41.clone.1), kind=kCustom, calls=%fused_computation.7 | custom fusion | flops 3145728 | bytes 12583424 | tf_op jit(solution)/shard_map/scatter-add | solution.py:55
  224.9 5.6 %convert_element_type.26 = bf16[1536,2048]{1,0:T(8,128)(2,1)S(1)} convert(f32[1536,2048]{1,0:T(8,128)} %scatter_custom_fusion) | non-fusion elementwise | flops 3145728 | bytes 18874368 | tf_op jit(solution)/shard_map/convert_element_type | solution.py:56
  230.4 0.0 copy-start
  230.4 74.2 %all_to_all.15 = bf16[8,192,2048]{2,1,0:T(8,128)(2,1)S(1)} all-to-all(bf16[8,192,2048]{2,1,0:T(8,128)(2,1)S(1)} %bitcast.61), channel_id=1, replica_groups=mesh['ez'=2,'ey'=2,'ex'=2] {'ez','ey','ex'}, dimensions={0} | all-to-all | bytes 12582912 | tf_op jit(solution)/shard_map/all_to_all | solution.py:57
  304.6 0.0 copy-done
  304.6 2.8 fusion.5
  (13 shorter events, 0.2 us)
Async XLA Ops:
  5.6 10.0 %all-to-all-start = ((f32[8,192,8]{1,2,0:T(8,128)}), f32[8,192,8]{1,2,0:T(8,128)S(1)}, u32[]{:S(2)}, u32[]{:S(2)}) async-start(f32[8,192,8]{1,2,0:T(8,128)} %copy.27), calls=%async_computation | async-start | bytes 131072 | tf_op jit(solution)/shard_map/all_to_all | solution.py:50
  15.6 7.7 %copy-start.2 = (s32[2]{0:T(128)S(1)}, s32[2]{0:T(128)}, u32[]{:S(2)}) copy-start(s32[2]{0:T(128)} %constant.45) | copy-start | bytes 28
  15.6 7.8 %copy-start.1 = (s32[2]{0:T(128)S(1)}, s32[2]{0:T(128)}, u32[]{:S(2)}) copy-start(s32[2]{0:T(128)} %constant.48) | copy-start | bytes 28
  15.6 99.8 %all-to-all-start.1 = ((bf16[8,192,2048]{2,1,0:T(8,128)(2,1)}), bf16[8,192,2048]{2,1,0:T(8,128)(2,1)}, u32[]{:S(2)}, u32[]{:S(2)}) async-start(bf16[8,192,2048]{2,1,0:T(8,128)(2,1)} %convolution_convert_fusion), calls=%async_computation.1 | async-start | bytes 12582912 | tf_op jit(solution)/shard_map/all_to_all | solution.py:49
  230.4 74.2 %copy-start = (bf16[256,2048]{1,0:T(8,128)(2,1)S(1)}, bf16[256,2048]{1,0:T(8,128)(2,1)}, u32[]{:S(2)}) copy-start(bf16[256,2048]{1,0:T(8,128)(2,1)} %param.6) | copy-start | bytes 3145732
where the time goes:
time: 308 us; the launch traced here: 307 us
  local copies, waits for them, and re-layouts  111 us (36%)
  matrix products  75.4 us (24%)
  blocking collectives  74.2 us (24%)
  other arithmetic  39.1 us (13%)
  starting transfers between devices  7.92 us (3%)
    all_to_all x1, blocking collectives, local_layer(): returned = lax.all_to_all(back_rows, ep_axes, 0, 0, tiled=True)  74.2 us
    unnamed x9, local copies, waits for them, and re-layouts  46 us
    another operation x1, local copies, waits for them, and re-layouts, local_layer(): jax.ops.segment_sum(weighted.reshape(-1, hidden), pick_rows.reshape(-1),...  45.6 us
    scatter-add x1, other arithmetic, local_layer(): jax.ops.segment_sum(weighted.reshape(-1, hidden), pick_rows.reshape(-1),...  26.4 us
    dot_general x1, matrix products, expert_ffn(): jnp.einsum('lch,lhf->lcf', x_pack, w_up, preferred_element_type=jnp.float32)  23.1 us
    dot_general x1, matrix products, expert_ffn(): jnp.einsum('lch,lhf->lcf', x_pack, w_gate, preferred_element_type=jnp.flo...  22.2 us
    dot_general x1, matrix products, expert_ffn(): jnp.einsum('lcf,lfh->lch', hidden_act, w_down, preferred_element_type=jnp...  21.5 us
    gather x1, local copies, waits for them, and re-layouts, local_layer(): flat_rows[pick_rows]  16.3 us
  transfers between devices with their start and end apart: 2, of which 0 were waited for; matrix products, arithmetic and copies ran while one was open for 33% of the time, Pallas kernels for 0%

commit v1 on v0

v1 whole, which is shorter than its diff:
```python
import functools
import math

import jax
import jax.numpy as jnp
from jax import lax
from jax.experimental import pallas as pl
from jax.experimental.pallas import tpu as pltpu
from jax.sharding import PartitionSpec as P

MESH = pl.DeviceIdType.MESH
F32 = jnp.float32
BF16 = jnp.bfloat16
RING = 4
RING2 = 2
CSUB = 4
HSUB = 8


def moe_kernel(dims, x_hbm, ids_hbm, gts_hbm, w1_hbm, w3_hbm, w2_hbm, y_hbm,
               xall, ids_all, gts_all, chosen_pos, pos_col, gate_tab, tok_tab, row_tab, gcol, xg, acc, hid, ring, ring2,
               psend, drecv, qsend, lrecv, ybuf, tok_sm, row_sm,
               loc_sem, tab_sem, rsend, rrecv, asend, arecv, wsem, w2sem, dsend, drsem, lsend, lrsem, ysem):
    tok, hidden, ff, n_loc, per_exp, topk = dims
    nc = hidden // (CSUB * 128)
    kc = CSUB * 128
    nh = hidden // (HSUB * 128)
    hc = HSUB * 128
    half = tok // 2
    n_dev = 8
    ct_ff = ff // 128
    zero_row = n_loc * per_exp
    xs = per_exp + 8

    z, y, c = lax.axis_index("ez"), lax.axis_index("ey"), lax.axis_index("ex")
    me = z * 4 + y * 2 + c
    xn, yn, pn = (z, 1 - y, c), (1 - z, y, c), (z, y, 1 - c)
    i_x = z * 4 + (1 - y) * 2 + c
    i_y = (1 - z) * 4 + y * 2 + c
    i_d = (1 - z) * 4 + (1 - y) * 2 + c

    def flip(i):
        b2, b1, b0 = (i >> 2) & 1, (i >> 1) & 1, i & 1
        t = (1 - z if b2 else z, 1 - y if b1 else y, 1 - c if b0 else c)
        return t, t[0] * 4 + t[1] * 2 + t[2]

    def w13_copies(k, e, slot):
        rows = pl.ds(k * kc, kc)
        return (pltpu.make_async_copy(w1_hbm.at[e, rows, :], ring.at[slot, 0], wsem.at[slot, 0]),
                pltpu.make_async_copy(w3_hbm.at[e, rows, :], ring.at[slot, 1], wsem.at[slot, 1]))

    def w2_copy(h, e, slot):
        return pltpu.make_async_copy(w2_hbm.at[e, :, pl.ds(h * hc, hc)], ring2.at[slot], w2sem.at[slot])

    own = pl.ds(pl.multiple_of(me * tok, tok), tok)
    loc = [pltpu.make_async_copy(x_hbm.at[k], xall[k].at[own], loc_sem.at[k]) for k in range(nc)]
    rlocs = [pltpu.make_async_copy(ids_hbm, ids_all.at[me], tab_sem.at[0]),
             pltpu.make_async_copy(gts_hbm, gts_all.at[me], tab_sem.at[3])]
    for cp in rlocs:
        cp.start()
    for cp in loc:
        cp.start()
    barrier = pltpu.get_barrier_semaphore()
    for i in range(1, n_dev):
        pl.semaphore_signal(barrier, inc=1, device_id=flip(i)[0], device_id_type=MESH)
    for e in range(RING):
        for cp in w13_copies(0, e, e):
            cp.start()
    pl.semaphore_wait(barrier, n_dev - 1)

    for cp in rlocs:
        cp.wait()
    rcopies = []
    for i in range(1, n_dev):
        for q, ref in enumerate((ids_all, gts_all)):
            cp = pltpu.make_async_remote_copy(ref.at[me], ref.at[me], rsend.at[q, i - 1], rrecv.at[q, i - 1],
                                              device_id=flip(i)[0], device_id_type=MESH)
            cp.start()
            rcopies.append(cp)

    def region(k, dev, lo, n):
        return xall[k].at[pl.ds(pl.multiple_of(dev * tok + lo, half), n)]

    partner_of = lambda d: d + 1 - 2 * c
    i_p = partner_of(me)
    flows = [
        (xn, me, i_x, 0, half), (xn, me, i_x, half, half), (xn, i_y, i_d, half, half),
        (yn, me, i_y, half, half), (yn, me, i_y, 0, half), (yn, i_x, i_d, 0, half),
        (pn, me, i_p, 0, tok),
        (pn, i_x, partner_of(i_x), 0, half), (pn, i_x, partner_of(i_x), half, half),
        (pn, i_y, partner_of(i_y), half, half), (pn, i_y, partner_of(i_y), 0, half),
        (pn, i_d, partner_of(i_d), 0, half), (pn, i_d, partner_of(i_d), half, half),
    ]

    def ag(k, n):
        tgt, src, _, lo, rows = flows[n]
        return pltpu.make_async_remote_copy(region(k, src, lo, rows), region(k, src, lo, rows),
                                            asend.at[k, n], arecv.at[k, n], device_id=tgt, device_id_type=MESH)

    def ag_recv(k, n):
        tgt, _, src, lo, rows = flows[n]
        pltpu.make_async_remote_copy(region(k, src, lo, rows), region(k, src, lo, rows),
                                     asend.at[k, n], arecv.at[k, n], device_id=tgt, device_id_type=MESH).wait_recv()

    def own_sends(k):
        for n in (0, 3, 1, 4, 6):
            ag(k, n).start()

    def relay1(k):
        ag_recv(k, 0)
        ag(k, 5).start()
        ag(k, 7).start()
        ag_recv(k, 3)
        ag(k, 2).start()
        ag(k, 9).start()

    def relay2(k):
        ag_recv(k, 1)
        ag(k, 8).start()
        ag_recv(k, 4)
        ag(k, 10).start()

    def relay3(k):
        ag_recv(k, 5)
        ag(k, 11).start()
        ag_recv(k, 2)
        ag(k, 12).start()

    def finish(k):
        for n in (6, 7, 9, 8, 10, 11, 12):
            ag_recv(k, n)

    for k in range(2):
        loc[k].wait()
        own_sends(k)
    for k in range(2, nc):
        loc[k].wait()

    for cp in rcopies:
        cp.wait()
    base = me * n_loc
    my_ids = lax.broadcasted_iota(jnp.int32, (n_loc, tok), 0) + base
    off = jnp.zeros((n_loc, 1), jnp.int32)
    for s in range(n_dev):
        ids_s = ids_all[s]
        gts_s = gts_all[s]
        hit = jnp.zeros((n_loc, tok), jnp.int32)
        gden = jnp.zeros((n_loc, tok), F32)
        for j in range(topk):
            m = ids_s[j:j + 1, :] == my_ids
            hit = jnp.where(m, 1, hit)
            gden = gden + jnp.where(m, gts_s[j:j + 1, :], 0.0)
        cum = hit
        step = 1
        while step < tok:
            cum = cum + jnp.concatenate([jnp.zeros((n_loc, step), jnp.int32), cum[:, 0:tok - step]], axis=1)
            step *= 2
        pos = off + cum - 1
        off = off + cum[:, tok - 1:tok]
        posm = jnp.where(hit > 0, pos, -1)
        chosen_pos[0:n_loc, s * tok:(s + 1) * tok] = posm
        gate_tab[0:n_loc, s * tok:(s + 1) * tok] = gden
        rows = jnp.full((8, tok), zero_row, jnp.int32)
        for e in range(n_loc):
            rows = jnp.where(ids_s == base + e, e * per_exp + pos[e:e + 1, :], rows)
        row_tab[:, s * tok:(s + 1) * tok] = rows
        pos_col[s * tok:(s + 1) * tok, 0:n_loc] = posm.T
    row_cp = pltpu.make_async_copy(row_tab, row_sm, tab_sem.at[1])
    row_cp.start()

    ipos = lax.broadcasted_iota(jnp.int32, (per_exp, tok), 0)
    lpos = lax.broadcasted_iota(jnp.int32, (tok, per_exp), 1)
    tcol = lax.broadcasted_iota(jnp.int32, (tok, per_exp), 0)
    for e in range(n_loc):
        def tok_step(s, tsum, e=e):
            pc = pos_col[pl.ds(pl.multiple_of(s * tok, tok), tok), e:e + 1]
            return tsum + jnp.where(pc == lpos, tcol + s * tok, 0)

        tsum = lax.fori_loop(0, n_dev, tok_step, jnp.zeros((tok, per_exp), jnp.int32))
        tok_tab[e:e + 1, 0:per_exp] = jnp.sum(tsum, axis=0, keepdims=True)

    def table_step(e, carry):
        gsum = jnp.zeros((per_exp, tok), F32)
        for s in range(n_dev):
            prow = chosen_pos[pl.ds(e, 1), s * tok:(s + 1) * tok]
            grow = gate_tab[pl.ds(e, 1), s * tok:(s + 1) * tok]
            gsum = gsum + jnp.where(prow == ipos, grow, 0.0)
        gcol[e] = jnp.broadcast_to(jnp.sum(gsum, axis=1, keepdims=True), (per_exp, 128))
        return carry

    lax.fori_loop(0, n_loc, table_step, 0)
    tok_cp = pltpu.make_async_copy(tok_tab.at[0:n_loc], tok_sm, tab_sem.at[2])
    tok_cp.start()

    relay1(0)
    relay2(0)
    if nc > 2:
        own_sends(2)
    row_cp.wait()
    tok_cp.wait()
    relay3(0)
    finish(0)

    def acc_row(e, mat, ct):
        return ((e * 2 + mat) * ct_ff + ct) * (per_exp // 8)

    def proj_step(k, e):
        slot = lax.rem(e, RING)

        def pick(i, carry):
            for u in range(8):
                r = i * 8 + u
                xg[pl.ds(r, CSUB, stride=xs), :] = xall[k][tok_sm[e, r]].astype(F32)
            return carry

        lax.fori_loop(0, per_exp // 8, pick, 0)
        for cp in w13_copies(k, e, slot):
            cp.wait()
        xe = jnp.concatenate([xg[ct * xs:ct * xs + per_exp, :] for ct in range(CSUB)], axis=1).astype(BF16)
        for ct in range(0, ct_ff, 2):
            w = min(2, ct_ff - ct)
            cols = slice(ct * 128, (ct + w) * 128)
            if w == 2:
                d = [jnp.dot(xe, ring[slot, mat, :, cols], preferred_element_type=F32) for mat in range(2)]
            else:
                both = jnp.concatenate([ring[slot, 0, :, cols], ring[slot, 1, :, cols]], axis=1)
                r = jnp.dot(xe, both, preferred_element_type=F32)
                d = [r[:, 0:128], r[:, 128:256]]
            for q in range(w):
                parts = []
                for mat in range(2):
                    at = pl.ds(acc_row(e, mat, ct + q), per_exp // 8)
                    v = d[mat][:, q * 128:(q + 1) * 128]
                    if k > 0:
                        v = v + acc[at].reshape(per_exp, 128)
                    if k < nc - 1:
                        acc[at] = v.reshape(per_exp // 8, 8, 128)
                    parts.append(v)
                if k == nc - 1:
                    hid[e, :, (ct + q) * 128:(ct + q + 1) * 128] = (jax.nn.silu(parts[0]) * parts[1]).astype(BF16)
        if k < nc - 1:
            @pl.when(e < n_loc - RING)
            def _():
                for cp in w13_copies(k, e + RING, slot):
                    cp.start()

            @pl.when(e >= n_loc - RING)
            def _():
                for cp in w13_copies(k + 1, e + RING - n_loc, slot):
                    cp.start()
        else:
            @pl.when(e < n_loc - RING)
            def _():
                for cp in w13_copies(k, e + RING, slot):
                    cp.start()

    for k in range(nc):
        if k == nc - 1:
            for e in range(RING2):
                w2_copy(0, e, e).start()

        def body(e, carry, k=k):
            proj_step(k, e)
            if k + 1 < nc:
                @pl.when(e == 1)
                def _():
                    relay1(k + 1)
                    relay2(k + 1)
                    if k + 3 < nc:
                        own_sends(k + 3)

                @pl.when(e == 5)
                def _():
                    relay3(k + 1)
            return carry

        lax.fori_loop(0, n_loc, body, 0)
        if k + 1 < nc:
            finish(k + 1)

    flat = acc.reshape(acc.shape[0] * 8, 128)

    def down(h):
        def body(e, carry):
            slot = lax.rem(e, RING2)
            w2_copy(h, e, slot).wait()
            g = gcol[e]
            for n in range(0, HSUB, 2):
                o = jnp.dot(hid[e], ring2[slot, :, n * 128:(n + 2) * 128], preferred_element_type=F32)
                for q in range(2):
                    flat[pl.ds(e * (per_exp * HSUB) + n + q, per_exp, stride=HSUB), :] = o[:, q * 128:(q + 1) * 128] * g

            @pl.when(e < n_loc - RING2)
            def _():
                w2_copy(h, e + RING2, slot).start()

            if h + 1 < nh:
                @pl.when(e >= n_loc - RING2)
                def _():
                    w2_copy(h + 1, e + RING2 - n_loc, slot).start()
            return carry

        lax.fori_loop(0, n_loc, body, 0)

    def token_sum(t):
        v = None
        for j in range(topk):
            r = acc[row_sm[j, t]]
            v = r if v is None else v + r
        return v

    def pair_sum(t):
        return jnp.concatenate([token_sum(t), token_sum(t + 1)], axis=0)

    pr = 2 * HSUB

    def each_pair(lo, n, fn):
        def body(i, carry):
            for u in range(2):
                fn(i * 2 + u)
            return carry
        lax.fori_loop(lo // 4, (lo + n) // 4, body, 0)

    def at_pair(i):
        return pl.ds(pl.multiple_of(i * pr, pr), pr)

    f_base = zero_row + 8
    qx_base = lambda h: f_base + h * half * 4
    qy_base = lambda h: qx_base(h) + half
    yo_base = lambda h: qx_base(h) + 2 * half

    def d2d(h, g):
        return pltpu.make_async_remote_copy(psend.at[h, g], drecv.at[h, g], dsend.at[h, g], drsem.at[h, g],
                                            device_id=pn, device_id_type=MESH)

    def link(h, n):
        return pltpu.make_async_remote_copy(qsend.at[h, n], lrecv.at[h, n], lsend.at[h, n], lrsem.at[h, n],
                                            device_id=xn if n in (0, 2, 4) else yn, device_id_type=MESH)

    groups = [i_d, i_x, i_y, me]

    def partner_group(h, g):
        t0 = partner_of(groups[g]) * tok

        def fn(i):
            psend[h, g, at_pair(i), :] = pair_sum(t0 + i * 2).astype(BF16)

        each_pair(0, tok, fn)
        d2d(h, g).start()

    def plane_sum(h, g, i):
        return pair_sum(groups[g] * tok + i * 2) + drecv[h, g, at_pair(i), :].astype(F32)

    def send_part(h, g, lo, n):
        def fn(i):
            qsend[h, n, at_pair(i - lo // 2), :] = plane_sum(h, g, i).astype(BF16)

        each_pair(lo, half, fn)
        link(h, n).start()

    def keep_part(h, g, lo, n, base):
        def fn(i):
            acc[pl.ds(base + i * 2 - lo, 2)] = plane_sum(h, g, i).reshape(2, HSUB, 128)

        each_pair(lo, n, fn)

    def relay_part(h, n, rn, base):
        link(h, rn).wait_recv()

        def fn(i):
            v = acc[pl.ds(base + i * 2, 2)].reshape(pr, 128)
            qsend[h, n, at_pair(i), :] = (v + lrecv[h, rn, at_pair(i), :].astype(F32)).astype(BF16)

        each_pair(0, half, fn)
        link(h, n).start()

    def combine_send(h):
        partner_group(h, 0)
        partner_group(h, 1)
        d2d(h, 0).wait_recv()
        send_part(h, 0, 0, 0)
        send_part(h, 0, half, 1)
        partner_group(h, 2)
        d2d(h, 1).wait_recv()
        send_part(h, 1, 0, 2)
        d2d(h, 2).wait_recv()
        send_part(h, 2, half, 3)
        keep_part(h, 1, half, half, qx_base(h))
        keep_part(h, 2, 0, half, qy_base(h))
        partner_group(h, 3)
        d2d(h, 3).wait_recv()
        keep_part(h, 3, 0, tok, yo_base(h))

    def combine_relay(h):
        relay_part(h, 4, 1, qx_base(h))
        relay_part(h, 5, 0, qy_base(h))

    def final(h):
        for n in (2, 3, 4, 5):
            link(h, n).wait_recv()
        for lo, n1, n2 in ((0, 2, 5), (half, 3, 4)):
            def fn(i, lo=lo, n1=n1, n2=n2):
                v = acc[pl.ds(yo_base(h) + i * 2 + lo, 2)].reshape(pr, 128)
                v = v + lrecv[h, n1, at_pair(i), :].astype(F32) + lrecv[h, n2, at_pair(i), :].astype(F32)
                for q in range(2):
                    t = (i * 2 + q) + lo
                    xr = jnp.concatenate([xall[h * (HSUB // CSUB) + m][me * tok + t] for m in range(HSUB // CSUB)], axis=0).astype(F32)
                    ybuf[t, h * HSUB:(h + 1) * HSUB, :] = (v[q * HSUB:(q + 1) * HSUB, :] + xr).astype(BF16)

            each_pair(0, half, fn)

    acc[zero_row] = jnp.zeros((HSUB, 128), F32)
    for h in range(nh):
        down(h)
        if h > 0:
            combine_relay(h - 1)
        combine_send(h)
    combine_relay(nh - 1)
    for h in range(nh):
        final(h)
    out = pltpu.make_async_copy(ybuf.at[0:tok], y_hbm, ysem.at[0])
    out.start()
    for k in range(nc):
        for n in range(13):
            ag(k, n).wait_send()
    for h in range(nh):
        for g in range(4):
            d2d(h, g).wait_send()
        for n in range(6):
            link(h, n).wait_send()
    out.wait()


def solution(mesh):
    ep_axes = tuple(mesh.axis_names)
    n_dev = math.prod(mesh.shape[a] for a in ep_axes)
    row_spec = P(ep_axes, None)
    w_spec = P(ep_axes, None, None)

    def local_layer(tokens, expert_ids, gate_weights, w_gate, w_up, w_down):
        tok, hidden = tokens.shape
        topk = expert_ids.shape[1]
        n_loc, _, ff = w_gate.shape
        per_exp = n_dev * tok * topk // (n_dev * n_loc)
        kc, hc = CSUB * 128, HSUB * 128
        nc, nh = hidden // kc, hidden // hc
        n_tok = n_dev * tok
        xt = tokens.reshape(tok, nc, CSUB, 128).transpose(1, 0, 2, 3)
        pad = ((0, 8 - topk), (0, 0))
        ids_t = jnp.pad(expert_ids.T, pad, constant_values=-1)
        gts_t = jnp.pad(gate_weights.T, pad)
        half = tok // 2
        acc_rows = max(2 * n_loc * per_exp * (ff // 128), (n_loc * per_exp + 8) * HSUB + nh * 4 * half * HSUB)
        dims = (tok, hidden, ff, n_loc, per_exp, topk)
        scratch = [
            [pltpu.VMEM((n_tok + 8, CSUB, 128), BF16) for _ in range(nc)],
            pltpu.VMEM((n_dev, 8, tok), jnp.int32),
            pltpu.VMEM((n_dev, 8, tok), F32),
            pltpu.VMEM((n_loc + 8, n_tok), jnp.int32),
            pltpu.VMEM((n_tok, 128), jnp.int32),
            pltpu.VMEM((n_loc + 8, n_tok), F32),
            pltpu.VMEM((n_loc + 8, 256), jnp.int32),
            pltpu.VMEM((8, n_tok), jnp.int32),
            pltpu.VMEM((n_loc, per_exp, 128), F32),
            pltpu.VMEM((8 * (per_exp + 8), 128), F32),
            pltpu.VMEM((acc_rows // 8, 8, 128), F32),
            pltpu.VMEM((n_loc, per_exp, ff), BF16),
            pltpu.VMEM((RING, 2, kc, ff), BF16),
            pltpu.VMEM((RING2, ff, hc), BF16),
            pltpu.VMEM((nh, 4, tok * HSUB, 128), BF16),
            pltpu.VMEM((nh, 4, tok * HSUB, 128), BF16),
            pltpu.VMEM((nh, 6, half * HSUB, 128), BF16),
            pltpu.VMEM((nh, 6, half * HSUB, 128), BF16),
            pltpu.VMEM((tok + 1, hidden // 128, 128), BF16),
            pltpu.SMEM((n_loc, 256), jnp.int32),
            pltpu.SMEM((8, n_tok), jnp.int32),
            pltpu.SemaphoreType.DMA((nc,)),
            pltpu.SemaphoreType.DMA((4,)),
            pltpu.SemaphoreType.DMA((2, n_dev - 1)),
            pltpu.SemaphoreType.DMA((2, n_dev - 1)),
            pltpu.SemaphoreType.DMA((nc, 13)),
            pltpu.SemaphoreType.DMA((nc, 13)),
            pltpu.SemaphoreType.DMA((RING, 2)),
            pltpu.SemaphoreType.DMA((RING2,)),
            pltpu.SemaphoreType.DMA((nh, 4)),
            pltpu.SemaphoreType.DMA((nh, 4)),
            pltpu.SemaphoreType.DMA((nh, 6)),
            pltpu.SemaphoreType.DMA((nh, 6)),
            pltpu.SemaphoreType.DMA((1,)),
        ]
        out = pl.pallas_call(
            functools.partial(moe_kernel, dims),
            out_shape=jax.ShapeDtypeStruct((tok, hidden // 128, 128), BF16),
            in_specs=[pl.BlockSpec(memory_space=pl.ANY)] * 6,
            out_specs=pl.BlockSpec(memory_space=pl.ANY),
            scratch_shapes=scratch,
            compiler_params=pltpu.CompilerParams(collective_id=0, has_side_effects=True,
                                                 vmem_limit_bytes=67043328),
        )(xt, ids_t, gts_t, w_gate, w_up, w_down)
        return out.reshape(tok, hidden)

    return jax.shard_map(local_layer, mesh=mesh, in_specs=(row_spec, row_spec, row_spec, w_spec, w_spec, w_spec), out_specs=row_spec, check_vma=False)
```

time: 308 us -> 163 us (0.53)
  Pallas kernels: 0 us -> 154 us
  local copies, waits for them, and re-layouts: 111 us -> 7.92 us
  matrix products: 75.4 us -> 0 us
  blocking collectives: 74.2 us -> 0 us
  other arithmetic: 39.1 us -> 0 us
  starting transfers between devices: 7.92 us -> 0 us
    pallas_call x0 -> x1, Pallas kernels: none -> 154 us  [local_layer(): pl.pallas_call(functools.partial(moe_kernel, dims), out_shape=jax.ShapeDt...]
    dot_general x5 -> x0, matrix products: 75.4 us -> none  [the longest x1 23.1 us: expert_ffn(): jnp.einsum('lch,lhf->lcf', x_pack, w_up, preferred_element_type=jnp.float32)]
    all_to_all x1 -> x0, blocking collectives: 74.2 us -> none  [local_layer(): returned = lax.all_to_all(back_rows, ep_axes, 0, 0, tiled=True)]
    another operation x4 -> x0, local copies, waits for them, and re-layouts: 45.9 us -> none  [the longest x1 45.6 us: local_layer(): jax.ops.segment_sum(weighted.reshape(-1, hidden), pick_rows.reshape(-1),...]
    unnamed x9 -> x2, local copies, waits for them, and re-layouts: 46 us -> 3.94 us
    scatter-add x1 -> x0, other arithmetic: 26.4 us -> none  [local_layer(): jax.ops.segment_sum(weighted.reshape(-1, hidden), pick_rows.reshape(-1),...]
    gather x1 -> x0, local copies, waits for them, and re-layouts: 16.3 us -> none  [local_layer(): flat_rows[pick_rows]]
    all_to_all x2 -> x0, starting transfers between devices: 7.92 us -> none  [the longest x1 4.3 us: local_layer(): recv_gates = lax.all_to_all(send_gates, ep_axes, 0, 0, tiled=True)]
  transfers between devices with their start and end apart: 2 -> 0, of which waited for: 0 -> 0; matrix products, arithmetic and copies ran while one was open for 33% -> 0% of each run, Pallas kernels for 0% -> 0%
where the time goes in v1:
time: 163 us; the launch traced here: 162 us
  Pallas kernels  154 us (94%)
  local copies, waits for them, and re-layouts  7.92 us (5%)
    pallas_call x1, Pallas kernels, local_layer(): pl.pallas_call(functools.partial(moe_kernel, dims), out_shape=jax.ShapeDt...  154 us
    unnamed x2, local copies, waits for them, and re-layouts  3.94 us

profile of v1, /device:TPU:0, one launch (start us, length us, event | category | flops | bytes accessed | tf_op | source)
XLA Modules:
  0.0 162.4 jit_solution(13429754425008042379)
XLA Ops:
  0.0 1.3 pad.8.ids_hbm
  1.3 1.3 pad.9.gts_hbm
  2.6 1.5 copy.7
  4.1 1.4 copy.8
  5.5 154.5 %shard_map.64 = bf16[256,16,128]{2,1,0:T(8,128)(2,1)} custom-call(bf16[4,256,4,128]{3,2,1,0:T(4,128)(2,1)} %bitcast.8, s32[8,256]{1,0:T(8,128)} %pad.8.ids_hbm, f32[8,256]{1,0:T(8,128)} %pad.9.gts_hbm, bf16[8,2048,1408]{2,1,0:T(8,128)(2,1)} %w1_hbm.1, bf16[8,2048,1408]{2,1,0:T(8,128)(2,1)} %w3_hbm.1, bf16[8,1408,2048]{2,1,0:T(8,128)(2,1)} %w2_hbm.1), custom_call_target="tpu_custom_call" | custom-call | tf_op jit(solution)/shard_map/pallas_call | solution.py:491
  160.0 2.5 %copy.11 = bf16[32,8,16,128]{3,1,2,0:T(8,128)(2,1)} copy(bf16[32,8,16,128]{3,2,1,0:T(8,128)(2,1)} %bitcast.9) | data formatting | bytes 2097152

commit v2 on v1

v2 whole, which is shorter than its diff:
```python
import functools
import math

import jax
import jax.numpy as jnp
from jax import lax
from jax.experimental import pallas as pl
from jax.experimental.pallas import tpu as pltpu
from jax.sharding import PartitionSpec as P

MESH = pl.DeviceIdType.MESH
F32 = jnp.float32
BF16 = jnp.bfloat16
RING = 5
CSUB = 4
HSUB = 8
TBLK = 64
TGRP = 4
UNROLL = 8


def unrolled(n, fn):
    def body(i, carry):
        fn(jnp.minimum(i, n - 1))
        return carry
    lax.fori_loop(0, n + 1, body, 0, unroll=n)


def moe_kernel(dims, x_hbm, ids_hbm, gts_hbm, w1_hbm, w3_hbm, w2_hbm, y_hbm,
               xall, ids_all, gts_all, chosen_pos, gate_tab, tok_tab, row_tab, pos_col, xg, xb, acc, hid, ring,
               psend, drecv, qsend, lrecv, ybuf, tok_sm, win_p, win_m, row_ord,
               loc_sem, tab_sem, rsend, rrecv, asend, arecv, wsem, dsend, drsem, lsend, lrsem, ysem, row_sem):
    tok, hidden, ff, n_loc, per_exp, topk = dims
    nc = hidden // (CSUB * 128)
    kc = CSUB * 128
    nh = hidden // (HSUB * 128)
    hc = HSUB * 128
    half = tok // 2
    n_dev = 8
    ct_ff = ff // 128
    zero_row = n_loc * per_exp
    xs = per_exp + 8

    z, y, c = lax.axis_index("ez"), lax.axis_index("ey"), lax.axis_index("ex")
    me = z * 4 + y * 2 + c
    xn, yn, pn = (z, 1 - y, c), (1 - z, y, c), (z, y, 1 - c)
    i_x = z * 4 + (1 - y) * 2 + c
    i_y = (1 - z) * 4 + y * 2 + c
    i_d = (1 - z) * 4 + (1 - y) * 2 + c

    def flip(i):
        b2, b1, b0 = (i >> 2) & 1, (i >> 1) & 1, i & 1
        t = (1 - z if b2 else z, 1 - y if b1 else y, 1 - c if b0 else c)
        return t, t[0] * 4 + t[1] * 2 + t[2]

    tail = ff - hc

    def w13_copies(k, e, slot):
        out = []
        for m, w in enumerate((w1_hbm, w3_hbm)):
            rows = pl.ds(k * kc, kc)
            out.append(pltpu.make_async_copy(w.at[e, rows, pl.ds(0, hc)], ring.at[slot, pl.ds(m * kc, kc), pl.ds(0, hc)], wsem.at[slot, 2 * m]))
            out.append(pltpu.make_async_copy(w.at[e, rows, pl.ds(hc, tail)], ring.at[slot, pl.ds(2 * kc, kc), pl.ds(m * tail, tail)],
                                             wsem.at[slot, 2 * m + 1]))
        return out

    def w2_copy(h, e, slot):
        return pltpu.make_async_copy(w2_hbm.at[e, :, pl.ds(pl.multiple_of(h * hc, hc), hc)], ring.at[slot, pl.ds(0, ff)],
                                     wsem.at[slot, 0])

    def weight(slot, m, ct, w):
        if ct * 128 < hc:
            return ring[slot, m * kc:(m + 1) * kc, ct * 128:(ct + w) * 128]
        c0 = m * tail + ct * 128 - hc
        return ring[slot, 2 * kc:3 * kc, c0:c0 + w * 128]

    own = pl.ds(pl.multiple_of(me * tok, tok), tok)
    loc = [pltpu.make_async_copy(x_hbm.at[pl.ds(0, tok), pl.ds(k * hc, hc)], ring.at[RING - 1, pl.ds(k * tok, tok)], loc_sem.at[k])
           for k in range(nh)]
    rlocs = [pltpu.make_async_copy(ids_hbm, ids_all.at[me], tab_sem.at[0]),
             pltpu.make_async_copy(gts_hbm, gts_all.at[me], tab_sem.at[3])]
    for cp in rlocs:
        cp.start()
    for cp in loc:
        cp.start()
    barrier = pltpu.get_barrier_semaphore()
    for i in range(1, n_dev):
        pl.semaphore_signal(barrier, inc=1, device_id=flip(i)[0], device_id_type=MESH)
    for e in range(RING - 1):
        for cp in w13_copies(0, e, e):
            cp.start()

    def own_rows(k):
        at = k * CSUB // HSUB
        for ct in range(CSUB):
            col = (k * CSUB + ct) % HSUB * 128
            xg[pl.ds(ct, tok, stride=CSUB), :] = ring[RING - 1, at * tok:(at + 1) * tok, col:col + 128].astype(F32)

        def one(t):
            xall[k][me * tok + t] = xg[pl.ds(pl.multiple_of(t * CSUB, CSUB), CSUB), :].astype(BF16)

        unrolled(tok, one)

    loc[0].wait()
    own_rows(0)
    pl.semaphore_wait(barrier, n_dev - 1)

    for cp in rlocs:
        cp.wait()
    rcopies = []
    for i in range(1, n_dev):
        for q, ref in enumerate((ids_all, gts_all)):
            cp = pltpu.make_async_remote_copy(ref.at[me], ref.at[me], rsend.at[q, i - 1], rrecv.at[q, i - 1],
                                              device_id=flip(i)[0], device_id_type=MESH)
            cp.start()
            rcopies.append(cp)

    def region(k, dev, lo, n):
        return xall[k].at[pl.ds(pl.multiple_of(dev * tok + lo, half), n)]

    partner_of = lambda d: d + 1 - 2 * c
    i_p = partner_of(me)
    flows = [
        (xn, me, i_x, 0, half), (xn, me, i_x, half, half), (xn, i_y, i_d, half, half),
        (yn, me, i_y, half, half), (yn, me, i_y, 0, half), (yn, i_x, i_d, 0, half),
        (pn, me, i_p, 0, tok),
        (pn, i_x, partner_of(i_x), 0, half), (pn, i_x, partner_of(i_x), half, half),
        (pn, i_y, partner_of(i_y), half, half), (pn, i_y, partner_of(i_y), 0, half),
        (pn, i_d, partner_of(i_d), 0, half), (pn, i_d, partner_of(i_d), half, half),
    ]

    def ag(k, n):
        tgt, src, _, lo, rows = flows[n]
        return pltpu.make_async_remote_copy(region(k, src, lo, rows), region(k, src, lo, rows),
                                            asend.at[k, n], arecv.at[k, n], device_id=tgt, device_id_type=MESH)

    def ag_recv(k, n):
        tgt, _, src, lo, rows = flows[n]
        pltpu.make_async_remote_copy(region(k, src, lo, rows), region(k, src, lo, rows),
                                     asend.at[k, n], arecv.at[k, n], device_id=tgt, device_id_type=MESH).wait_recv()

    def own_sends(k):
        for n in (0, 3, 1, 4, 6):
            ag(k, n).start()

    def relay1(k):
        ag_recv(k, 0)
        ag(k, 5).start()
        ag(k, 7).start()
        ag_recv(k, 3)
        ag(k, 2).start()
        ag(k, 9).start()

    def relay2(k):
        ag_recv(k, 1)
        ag(k, 8).start()
        ag_recv(k, 4)
        ag(k, 10).start()

    def relay3(k):
        ag_recv(k, 5)
        ag(k, 11).start()
        ag_recv(k, 2)
        ag(k, 12).start()

    def finish(k):
        for n in (6, 7, 9, 8, 10, 11, 12):
            ag_recv(k, n)

    own_sends(0)
    for k in range(1, nc):
        if k * CSUB % HSUB == 0:
            loc[k * CSUB // HSUB].wait()
        own_rows(k)
    for cp in w13_copies(0, RING - 1, RING - 1):
        cp.start()

    for cp in rcopies:
        cp.wait()
    base = me * n_loc
    my_ids = lax.broadcasted_iota(jnp.int32, (n_loc, tok), 0) + base
    off = jnp.zeros((n_loc, 1), jnp.int32)
    for s in range(n_dev):
        ids_s = ids_all[s]
        gts_s = gts_all[s]
        hit = jnp.zeros((n_loc, tok), jnp.int32)
        gden = jnp.zeros((n_loc, tok), F32)
        for j in range(topk):
            m = ids_s[j:j + 1, :] == my_ids
            hit = jnp.where(m, 1, hit)
            gden = gden + jnp.where(m, gts_s[j:j + 1, :], 0.0)
        cum = hit
        step = 1
        while step < tok:
            cum = cum + jnp.concatenate([jnp.zeros((n_loc, step), jnp.int32), cum[:, 0:tok - step]], axis=1)
            step *= 2
        pos = off + cum - 1
        off = off + cum[:, tok - 1:tok]
        posm = jnp.where(hit > 0, pos, -1)
        chosen_pos[s] = posm
        pos_col[s * tok:(s + 1) * tok, 0:n_loc] = posm.T
        gate_tab[s] = gden
        rows = jnp.full((topk, tok), zero_row, jnp.int32)
        for e in range(n_loc):
            rows = jnp.where(ids_s == base + e, e * per_exp + pos[e:e + 1, :], rows)
        for q in range(tok // 128):
            at = (s * (tok // 128) + q) * 8
            row_tab[at:at + topk, :] = rows[:, q * 128:(q + 1) * 128]
            row_tab[at + topk:at + 8, :] = jnp.zeros((8 - topk, 128), jnp.int32)
    order = [(i_d, 0), (i_d, 1), (i_x, 0), (i_y, 1), (i_x, 1), (i_y, 0), (me, 0), (me, 1)]
    n_blk = len(order)
    for b, (dev, hf) in enumerate(order):
        for side, d in enumerate((partner_of(dev), dev)):
            row_ord[side, b] = row_tab[pl.ds(pl.multiple_of((d * 2 + hf) * 8, 8), 8), :]

    def window(side, b):
        return pltpu.make_async_copy(row_ord.at[side, b], (win_p, win_m)[side], row_sem.at[side])

    relay1(0)
    own_sends(1)
    relay2(0)
    lpos = lax.broadcasted_iota(jnp.int32, (TBLK, per_exp), 1)
    tcol = lax.broadcasted_iota(jnp.int32, (TBLK, per_exp), 0)
    for e0 in range(0, n_loc, TGRP):
        def tok_step(i, sums, e0=e0):
            pc = pos_col[pl.ds(pl.multiple_of(i * TBLK, TBLK), TBLK), :]
            out = []
            for e in range(TGRP):
                hitv = jnp.where(pc[:, e0 + e:e0 + e + 1] == lpos, tcol + i * TBLK, 0)
                out.append(sums[e] + jnp.sum(hitv.reshape(TBLK // 8, 8, per_exp), axis=0))
            return tuple(out)

        sums = lax.fori_loop(0, n_dev * tok // TBLK, tok_step,
                             tuple(jnp.zeros((8, per_exp), jnp.int32) for _ in range(TGRP)))
        for e in range(TGRP):
            tok_tab[e0 + e:e0 + e + 1, 0:per_exp] = jnp.sum(sums[e], axis=0, keepdims=True)

    tok_cp = pltpu.make_async_copy(tok_tab.at[0:n_loc], tok_sm, tab_sem.at[2])
    tok_cp.start()

    relay3(0)

    tok_cp.wait()
    finish(0)

    def acc_row(e, mat, ct):
        return ((e * 2 + mat) * ct_ff + ct) * (per_exp // 8)

    def pick(k, e, lo, n):
        def one(i):
            xg[pl.ds(lo + i, CSUB, stride=xs), :] = xall[k][tok_sm[e, lo + i]].astype(F32)

        unrolled(n, one)

    def proj_step(k, e):
        slot = lax.rem(k * n_loc + e, RING)
        for cp in w13_copies(k, e, slot):
            cp.wait()
        for ct in range(CSUB):
            xb[:, ct * 128:(ct + 1) * 128] = xg[ct * xs:ct * xs + per_exp, :].astype(BF16)
        nxt = jnp.minimum(e + 1, n_loc - 1)
        steps = list(range(0, ct_ff, 2))
        share = per_exp // len(steps)
        for si, ct in enumerate(steps):
            w = min(2, ct_ff - ct)
            if w == 2:
                d = [jnp.dot(xb[...], weight(slot, mat, ct, w), preferred_element_type=F32) for mat in range(2)]
            else:
                both = jnp.concatenate([weight(slot, mat, ct, w) for mat in range(2)], axis=1)
                r = jnp.dot(xb[...], both, preferred_element_type=F32)
                d = [r[:, 0:128], r[:, 128:256]]
            pick(k, nxt, si * share, share)
            for q in range(w):
                parts = []
                for mat in range(2):
                    at = pl.ds(acc_row(e, mat, ct + q), per_exp // 8)
                    v = d[mat][:, q * 128:(q + 1) * 128]
                    if k > 0:
                        v = v + acc[at].reshape(per_exp, 128)
                    if k < nc - 1:
                        acc[at] = v.reshape(per_exp // 8, 8, 128)
                    parts.append(v)
                if k == nc - 1:
                    hid[e, :, (ct + q) * 128:(ct + q + 1) * 128] = (jax.nn.silu(parts[0]) * parts[1]).astype(BF16)
        @pl.when(e < n_loc - RING)
        def _():
            for cp in w13_copies(k, e + RING, slot):
                cp.start()

        @pl.when(e >= n_loc - RING)
        def _():
            if k < nc - 1:
                for cp in w13_copies(k + 1, e + RING - n_loc, slot):
                    cp.start()
            else:
                w2_copy(0, e + RING - n_loc, slot).start()

    for k in range(nc):
        pick(k, 0, 0, per_exp)

        def body(e, carry, k=k):
            proj_step(k, e)
            if k + 1 < nc:
                @pl.when(e == 1)
                def _():
                    relay1(k + 1)
                    if k + 2 < nc:
                        own_sends(k + 2)

                @pl.when(e == 4)
                def _():
                    relay2(k + 1)

                @pl.when(e == 6)
                def _():
                    relay3(k + 1)
            return carry

        lax.fori_loop(0, n_loc, body, 0)
        if k + 1 < nc:
            finish(k + 1)

    flat = acc.reshape(acc.shape[0] * 8, 128)

    def down(h):
        def body(e, carry):
            step = h * n_loc + e
            slot = lax.rem(nc * n_loc + step, RING)
            w2_copy(h, e, slot).wait()
            ipos = lax.broadcasted_iota(jnp.int32, (per_exp, tok), 0)
            gsum = jnp.zeros((per_exp, tok), F32)
            for s in range(n_dev):
                prow = chosen_pos[s, pl.ds(e, 1), :]
                grow = gate_tab[s, pl.ds(e, 1), :]
                gsum = gsum + jnp.where(prow == ipos, grow, 0.0)
            g = jnp.broadcast_to(jnp.sum(gsum, axis=1, keepdims=True), (per_exp, 128))
            for n in range(0, HSUB, 2):
                o = jnp.dot(hid[e], ring[slot, 0:ff, n * 128:(n + 2) * 128], preferred_element_type=F32)
                for q in range(2):
                    flat[pl.ds(e * (per_exp * HSUB) + n + q, per_exp, stride=HSUB), :] = o[:, q * 128:(q + 1) * 128] * g

            @pl.when(e < n_loc - RING)
            def _():
                w2_copy(h, e + RING, slot).start()

            @pl.when(jnp.logical_and(e >= n_loc - RING, h < nh - 1))
            def _():
                w2_copy(h + 1, e + RING - n_loc, slot).start()

            return carry

        lax.fori_loop(0, n_loc, body, 0)

    def pair_sum(win, i):
        out = []
        for t in (2 * i, 2 * i + 1):
            v = acc[win[0, t]]
            for j in range(1, topk):
                v = v + acc[win[j, t]]
            out.append(v)
        return jnp.concatenate(out, axis=0)

    pr = 2 * HSUB
    f_base = zero_row + 8

    def at_pair(i):
        return pl.ds(i * pr if isinstance(i, int) else pl.multiple_of(i * pr, pr), pr)

    def kept(h, b):
        return f_base + (h * n_blk + b) * half

    def d2d(h, b):
        return pltpu.make_async_remote_copy(psend.at[h, b], drecv.at[h, b], dsend.at[h, b], drsem.at[h, b],
                                            device_id=pn, device_id_type=MESH)

    def link(h, n):
        par = n % 2 if isinstance(n, int) else lax.rem(n, 2)
        tgt = (z + par * (1 - 2 * z), y + (1 - par) * (1 - 2 * y), c)
        return pltpu.make_async_remote_copy(qsend.at[h, n], lrecv.at[h, n], lsend.at[h, n], lrsem.at[h, n],
                                            device_id=tgt, device_id_type=MESH)

    def pairs(fn):
        def body(i, carry):
            for u in range(UNROLL):
                fn(i * UNROLL + u)
            return carry
        lax.fori_loop(0, half // (2 * UNROLL), body, 0)

    def relay_part(h, n, rn, base):
        link(h, rn).wait_recv()

        def fn(i):
            v = acc[pl.ds(base + i * 2, 2)].reshape(pr, 128)
            qsend[h, n, at_pair(i), :] = (v + lrecv[h, rn, at_pair(i), :].astype(F32)).astype(BF16)

        pairs(fn)
        link(h, n).start()

    def combine_send(h):
        def body(b, carry):
            @pl.when(b < n_blk)
            def _():
                window(0, b).wait()

                def part(i):
                    psend[h, b, at_pair(i), :] = pair_sum(win_p, i).astype(BF16)

                unrolled(half // 2, part)
                d2d(h, b).start()

                @pl.when(b < n_blk - 1)
                def _():
                    window(0, b + 1).start()

            @pl.when(b > 0)
            def _():
                m = b - 1
                d2d(h, m).wait_recv()
                window(1, m).wait()
                n = jnp.minimum(m, 5)

                def whole(i):
                    v = pair_sum(win_m, i) + drecv[h, m, at_pair(i), :].astype(F32)
                    qsend[h, n, at_pair(i), :] = v.astype(BF16)
                    acc[pl.ds(kept(h, m) + i * 2, 2)] = v.reshape(2, HSUB, 128)

                unrolled(half // 2, whole)

                @pl.when(m < n_blk - 1)
                def _():
                    window(1, m + 1).start()

                @pl.when(m < 4)
                def _():
                    link(h, m).start()

            return carry

        lax.fori_loop(0, n_blk + 1, body, 0)

    def combine_relay(h):
        relay_part(h, 4, 1, kept(h, 4))
        relay_part(h, 5, 0, kept(h, 5))

    def final(h):
        for n in (2, 3, 4, 5):
            link(h, n).wait_recv()
        for lo, n1, n2 in ((0, 2, 5), (half, 3, 4)):
            def fn(i, lo=lo, n1=n1, n2=n2):
                v = acc[pl.ds(kept(h, 6) + i * 2 + lo, 2)].reshape(pr, 128)
                v = v + lrecv[h, n1, at_pair(i), :].astype(F32) + lrecv[h, n2, at_pair(i), :].astype(F32)
                for q in range(2):
                    t = (i * 2 + q) + lo
                    xr = jnp.concatenate([xall[h * (HSUB // CSUB) + m][me * tok + t] for m in range(HSUB // CSUB)], axis=0).astype(F32)
                    ybuf[t, h * HSUB:(h + 1) * HSUB, :] = (v[q * HSUB:(q + 1) * HSUB, :] + xr).astype(BF16)

            pairs(fn)

    acc[zero_row] = jnp.zeros((HSUB, 128), F32)

    def half_step(h, carry):
        window(0, 0).start()
        window(1, 0).start()
        down(h)

        @pl.when(h > 0)
        def _():
            combine_relay(h - 1)

        combine_send(h)
        return carry

    lax.fori_loop(0, nh, half_step, 0)
    combine_relay(nh - 1)
    for h in range(nh):
        final(h)
    out = pltpu.make_async_copy(ybuf.at[0:tok], y_hbm, ysem.at[0])
    out.start()
    for k in range(nc):
        for n in range(13):
            ag(k, n).wait_send()
    for h in range(nh):
        for b in range(n_blk):
            d2d(h, b).wait_send()
        for n in range(6):
            link(h, n).wait_send()
    out.wait()


def solution(mesh):
    ep_axes = tuple(mesh.axis_names)
    n_dev = math.prod(mesh.shape[a] for a in ep_axes)
    row_spec = P(ep_axes, None)
    w_spec = P(ep_axes, None, None)

    def local_layer(tokens, expert_ids, gate_weights, w_gate, w_up, w_down):
        tok, hidden = tokens.shape
        topk = expert_ids.shape[1]
        n_loc, _, ff = w_gate.shape
        per_exp = n_dev * tok * topk // (n_dev * n_loc)
        kc, hc = CSUB * 128, HSUB * 128
        nc, nh = hidden // kc, hidden // hc
        n_tok = n_dev * tok
        half = tok // 2
        acc_rows = max(2 * n_loc * per_exp * (ff // 128), (n_loc * per_exp + 8) * HSUB + nh * 8 * half * HSUB)
        dims = (tok, hidden, ff, n_loc, per_exp, topk)
        scratch = [
            [pltpu.VMEM((n_tok + 8, CSUB, 128), BF16) for _ in range(nc)],
            pltpu.VMEM((n_dev, topk, tok), jnp.int32),
            pltpu.VMEM((n_dev, topk, tok), F32),
            pltpu.VMEM((n_dev + 1, n_loc, tok), jnp.int32),
            pltpu.VMEM((n_dev + 1, n_loc, tok), F32),
            pltpu.VMEM((n_loc + 8, 256), jnp.int32),
            pltpu.VMEM((n_tok // 16, 128), jnp.int32),
            pltpu.VMEM((n_tok, 128), jnp.int32),
            pltpu.VMEM((8 * (per_exp + 8), 128), F32),
            pltpu.VMEM((per_exp, kc), BF16),
            pltpu.VMEM((acc_rows // 8, 8, 128), F32),
            pltpu.VMEM((n_loc, per_exp, ff), BF16),
            pltpu.VMEM((RING, max(3 * kc, ff), hc), BF16),
            pltpu.VMEM((nh, 8, half * HSUB, 128), BF16),
            pltpu.VMEM((nh, 8, half * HSUB, 128), BF16),
            pltpu.VMEM((nh, 6, half * HSUB, 128), BF16),
            pltpu.VMEM((nh, 6, half * HSUB, 128), BF16),
            pltpu.VMEM((tok + 1, hidden // 128, 128), BF16),
            pltpu.SMEM((n_loc, 256), jnp.int32),
            pltpu.SMEM((8, 128), jnp.int32),
            pltpu.SMEM((8, 128), jnp.int32),
            pltpu.VMEM((2, 8, 8, 128), jnp.int32),
            pltpu.SemaphoreType.DMA((nc,)),
            pltpu.SemaphoreType.DMA((4,)),
            pltpu.SemaphoreType.DMA((2, n_dev - 1)),
            pltpu.SemaphoreType.DMA((2, n_dev - 1)),
            pltpu.SemaphoreType.DMA((nc, 13)),
            pltpu.SemaphoreType.DMA((nc, 13)),
            pltpu.SemaphoreType.DMA((RING, 4)),
            pltpu.SemaphoreType.DMA((nh, 8)),
            pltpu.SemaphoreType.DMA((nh, 8)),
            pltpu.SemaphoreType.DMA((nh, 6)),
            pltpu.SemaphoreType.DMA((nh, 6)),
            pltpu.SemaphoreType.DMA((1,)),
            pltpu.SemaphoreType.DMA((2,)),
        ]
        out = pl.pallas_call(
            functools.partial(moe_kernel, dims),
            out_shape=jax.ShapeDtypeStruct((tok, hidden // 128, 128), BF16),
            in_specs=[pl.BlockSpec(memory_space=pl.ANY)] * 6,
            out_specs=pl.BlockSpec(memory_space=pl.ANY),
            scratch_shapes=scratch,
            compiler_params=pltpu.CompilerParams(collective_id=0, has_side_effects=True,
                                                 vmem_limit_bytes=67043328),
        )(tokens, expert_ids.T, gate_weights.T, w_gate, w_up, w_down)
        return out.reshape(tok, hidden)

    return jax.shard_map(local_layer, mesh=mesh, in_specs=(row_spec, row_spec, row_spec, w_spec, w_spec, w_spec), out_specs=row_spec, check_vma=False)
```

time: 163 us -> 113 us (0.69)
  Pallas kernels: 154 us -> 111 us
  local copies, waits for them, and re-layouts: 7.92 us -> 2.47 us
    pallas_call x1, Pallas kernels: 154 us -> 111 us  [local_layer(): pl.pallas_call(functools.partial(moe_kernel, dims), out_shape=jax.ShapeDt...]
    pad x2 -> x0, local copies, waits for them, and re-layouts: 2.59 us -> none  [the longest x1 1.3 us: local_layer(): gts_t = jnp.pad(gate_weights.T, pad)]
    unnamed x2 -> x1, local copies, waits for them, and re-layouts: 3.94 us -> 2.47 us
where the time goes in v2:
time: 113 us
  Pallas kernels  111 us (98%)
  local copies, waits for them, and re-layouts  2.47 us (2%)
    pallas_call x1, Pallas kernels, local_layer(): pl.pallas_call(functools.partial(moe_kernel, dims), out_shape=jax.ShapeDt...  111 us
    unnamed x1, local copies, waits for them, and re-layouts  2.47 us

profile of v2, /device:TPU:0, one launch (start us, length us, event | category | flops | bytes accessed | tf_op | source)
XLA Modules:
  0.0 113.3 jit_solution(16967947362123407551)
XLA Ops:
  0.0 110.8 %shard_map.64 = bf16[256,16,128]{2,1,0:T(8,128)(2,1)} custom-call(bf16[256,2048]{1,0:T(8,128)(2,1)} %x_hbm.1, s32[6,256]{1,0:T(8,128)} %bitcast.7, f32[6,256]{1,0:T(8,128)} %bitcast.8, bf16[8,2048,1408]{2,1,0:T(8,128)(2,1)} %w1_hbm.1, bf16[8,2048,1408]{2,1,0:T(8,128)(2,1)} %w3_hbm.1, bf16[8,1408,2048]{2,1,0:T(8,128)(2,1)} %w2_hbm.1), custom_call_target="tpu_custom_call" | custom-call | tf_op jit(solution)/shard_map/pallas_call | solution.py:544
  110.8 2.5 %copy.9 = bf16[32,8,16,128]{3,1,2,0:T(8,128)(2,1)} copy(bf16[32,8,16,128]{3,2,1,0:T(8,128)(2,1)} %bitcast.6) | data formatting | bytes 2097152

commit v3 on v2

--- a/solution.py
+++ b/solution.py
@@ -205,7 +205,7 @@
             rows = jnp.where(ids_s == base + e, e * per_exp + pos[e:e + 1, :], rows)
         for q in range(tok // 128):
             at = (s * (tok // 128) + q) * 8
-            row_tab[at:at + topk, :] = rows[:, q * 128:(q + 1) * 128]
+            row_tab[at:at + topk, :] = rows[:, q * 128:(q + 1) * 128] * HSUB
             row_tab[at + topk:at + 8, :] = jnp.zeros((8 - topk, 128), jnp.int32)
     order = [(i_d, 0), (i_d, 1), (i_x, 0), (i_y, 1), (i_x, 1), (i_y, 0), (me, 0), (me, 1)]
     n_blk = len(order)
@@ -231,7 +231,7 @@
             return tuple(out)
 
         sums = lax.fori_loop(0, n_dev * tok // TBLK, tok_step,
-                             tuple(jnp.zeros((8, per_exp), jnp.int32) for _ in range(TGRP)))
+                             tuple(jnp.zeros((8, per_exp), jnp.int32) for _ in range(TGRP)), unroll=4)
         for e in range(TGRP):
             tok_tab[e0 + e:e0 + e + 1, 0:per_exp] = jnp.sum(sums[e], axis=0, keepdims=True)
 
@@ -242,6 +242,8 @@
 
     tok_cp.wait()
     finish(0)
+    relay1(1)
+    own_sends(2)
 
     def acc_row(e, mat, ct):
         return ((e * 2 + mat) * ct_ff + ct) * (per_exp // 8)
@@ -301,13 +303,14 @@
         def body(e, carry, k=k):
             proj_step(k, e)
             if k + 1 < nc:
-                @pl.when(e == 1)
-                def _():
-                    relay1(k + 1)
-                    if k + 2 < nc:
-                        own_sends(k + 2)
-
-                @pl.when(e == 4)
+                if k > 0:
+                    @pl.when(e == 1)
+                    def _():
+                        relay1(k + 1)
+                        if k + 2 < nc:
+                            own_sends(k + 2)
+
+                @pl.when(e == (4 if k > 0 else 1))
                 def _():
                     relay2(k + 1)
 
@@ -354,9 +357,9 @@
     def pair_sum(win, i):
         out = []
         for t in (2 * i, 2 * i + 1):
-            v = acc[win[0, t]]
+            v = flat[pl.ds(win[0, t], HSUB), :]
             for j in range(1, topk):
-                v = v + acc[win[j, t]]
+                v = v + flat[pl.ds(win[j, t], HSUB), :]
             out.append(v)
         return jnp.concatenate(out, axis=0)
 
@@ -396,6 +399,10 @@
         pairs(fn)
         link(h, n).start()
 
+    def combine_relay(h):
+        relay_part(h, 4, 1, kept(h, 4))
+        relay_part(h, 5, 0, kept(h, 5))
+
     def combine_send(h):
         def body(b, carry):
             @pl.when(b < n_blk)
@@ -417,7 +424,7 @@
                 m = b - 1
                 d2d(h, m).wait_recv()
                 window(1, m).wait()
-                n = jnp.minimum(m, 5)
+                n = jnp.minimum(m, 6)
 
                 def whole(i):
                     v = pair_sum(win_m, i) + drecv[h, m, at_pair(i), :].astype(F32)
@@ -434,13 +441,13 @@
                 def _():
                     link(h, m).start()
 
+                @pl.when(m == n_blk - 1)
+                def _():
+                    combine_relay(h)
+
             return carry
 
         lax.fori_loop(0, n_blk + 1, body, 0)
-
-    def combine_relay(h):
-        relay_part(h, 4, 1, kept(h, 4))
-        relay_part(h, 5, 0, kept(h, 5))
 
     def final(h):
         for n in (2, 3, 4, 5):
@@ -463,19 +470,17 @@
         window(1, 0).start()
         down(h)
 
-        @pl.when(h > 0)
-        def _():
-            combine_relay(h - 1)
-
         combine_send(h)
         return carry
 
     lax.fori_loop(0, nh, half_step, 0)
-    combine_relay(nh - 1)
+    outs = []
     for h in range(nh):
         final(h)
-    out = pltpu.make_async_copy(ybuf.at[0:tok], y_hbm, ysem.at[0])
-    out.start()
+        out = pltpu.make_async_copy(ybuf.at[pl.ds(0, tok), pl.ds(h * HSUB, HSUB)], y_hbm.at[pl.ds(0, tok), pl.ds(h * HSUB, HSUB)],
+                                    ysem.at[h])
+        out.start()
+        outs.append(out)
     for k in range(nc):
         for n in range(13):
             ag(k, n).wait_send()
@@ -484,7 +489,8 @@
             d2d(h, b).wait_send()
         for n in range(6):
             link(h, n).wait_send()
-    out.wait()
+    for out in outs:
+        out.wait()
 
 
 def solution(mesh):
@@ -520,7 +526,7 @@
             pltpu.VMEM((RING, max(3 * kc, ff), hc), BF16),
             pltpu.VMEM((nh, 8, half * HSUB, 128), BF16),
             pltpu.VMEM((nh, 8, half * HSUB, 128), BF16),
-            pltpu.VMEM((nh, 6, half * HSUB, 128), BF16),
+            pltpu.VMEM((nh, 7, half * HSUB, 128), BF16),
             pltpu.VMEM((nh, 6, half * HSUB, 128), BF16),
             pltpu.VMEM((tok + 1, hidden // 128, 128), BF16),
             pltpu.SMEM((n_loc, 256), jnp.int32),
@@ -538,7 +544,7 @@
             pltpu.SemaphoreType.DMA((nh, 8)),
             pltpu.SemaphoreType.DMA((nh, 6)),
             pltpu.SemaphoreType.DMA((nh, 6)),
-            pltpu.SemaphoreType.DMA((1,)),
+            pltpu.SemaphoreType.DMA((nh,)),
             pltpu.SemaphoreType.DMA((2,)),
         ]
         out = pl.pallas_call(

time: 113 us -> 107 us (0.947)
  Pallas kernels: 111 us -> 105 us
    pallas_call x1, Pallas kernels: 111 us -> 105 us  [local_layer(): pl.pallas_call(functools.partial(moe_kernel, dims), out_shape=jax.ShapeDt...]
where the time goes in v3:
time: 107 us
  Pallas kernels  105 us (98%)
  local copies, waits for them, and re-layouts  2.47 us (2%)
    pallas_call x1, Pallas kernels, local_layer(): pl.pallas_call(functools.partial(moe_kernel, dims), out_shape=jax.ShapeDt...  105 us
    unnamed x1, local copies, waits for them, and re-layouts  2.47 us

profile of v3, /device:TPU:0, one launch (start us, length us, event | category | flops | bytes accessed | tf_op | source)
XLA Modules:
  0.0 107.3 jit_solution(17126503371694651022)
XLA Ops:
  0.0 104.9 %shard_map.64 = bf16[256,16,128]{2,1,0:T(8,128)(2,1)} custom-call(bf16[256,2048]{1,0:T(8,128)(2,1)} %x_hbm.1, s32[6,256]{1,0:T(8,128)} %bitcast.7, f32[6,256]{1,0:T(8,128)} %bitcast.8, bf16[8,2048,1408]{2,1,0:T(8,128)(2,1)} %w1_hbm.1, bf16[8,2048,1408]{2,1,0:T(8,128)(2,1)} %w3_hbm.1, bf16[8,1408,2048]{2,1,0:T(8,128)(2,1)} %w2_hbm.1), custom_call_target="tpu_custom_call" | custom-call | tf_op jit(solution)/shard_map/pallas_call | solution.py:550
  104.9 2.5 %copy.9 = bf16[32,8,16,128]{3,1,2,0:T(8,128)(2,1)} copy(bf16[32,8,16,128]{3,2,1,0:T(8,128)(2,1)} %bitcast.6) | data formatting | bytes 2097152

commit v4 on v3

--- a/solution.py
+++ b/solution.py
@@ -27,7 +27,7 @@
 
 
 def moe_kernel(dims, x_hbm, ids_hbm, gts_hbm, w1_hbm, w3_hbm, w2_hbm, y_hbm,
-               xall, ids_all, gts_all, chosen_pos, gate_tab, tok_tab, row_tab, pos_col, xg, xb, acc, hid, ring,
+               xall, ids_all, gts_all, chosen_pos, gate_tab, tok_tab, row_tab, pos_col, gcol, xg, xb, acc, hid, ring,
                psend, drecv, qsend, lrecv, ybuf, tok_sm, win_p, win_m, row_ord,
                loc_sem, tab_sem, rsend, rrecv, asend, arecv, wsem, dsend, drsem, lsend, lrsem, ysem, row_sem):
     tok, hidden, ff, n_loc, per_exp, topk = dims
@@ -254,6 +254,15 @@
 
         unrolled(n, one)
 
+    def gate_column(e):
+        ipos = lax.broadcasted_iota(jnp.int32, (per_exp, tok), 0)
+        gsum = jnp.zeros((per_exp, tok), F32)
+        for s in range(n_dev):
+            prow = chosen_pos[s, pl.ds(e, 1), :]
+            grow = gate_tab[s, pl.ds(e, 1), :]
+            gsum = gsum + jnp.where(prow == ipos, grow, 0.0)
+        gcol[e] = jnp.broadcast_to(jnp.sum(gsum, axis=1, keepdims=True), (per_exp, 128))
+
     def proj_step(k, e):
         slot = lax.rem(k * n_loc + e, RING)
         for cp in w13_copies(k, e, slot):
@@ -261,6 +270,8 @@
         for ct in range(CSUB):
             xb[:, ct * 128:(ct + 1) * 128] = xg[ct * xs:ct * xs + per_exp, :].astype(BF16)
         nxt = jnp.minimum(e + 1, n_loc - 1)
+        if k == 1:
+            gate_column(e)
         steps = list(range(0, ct_ff, 2))
         share = per_exp // len(steps)
         for si, ct in enumerate(steps):
@@ -330,13 +341,7 @@
             step = h * n_loc + e
             slot = lax.rem(nc * n_loc + step, RING)
             w2_copy(h, e, slot).wait()
-            ipos = lax.broadcasted_iota(jnp.int32, (per_exp, tok), 0)
-            gsum = jnp.zeros((per_exp, tok), F32)
-            for s in range(n_dev):
-                prow = chosen_pos[s, pl.ds(e, 1), :]
-                grow = gate_tab[s, pl.ds(e, 1), :]
-                gsum = gsum + jnp.where(prow == ipos, grow, 0.0)
-            g = jnp.broadcast_to(jnp.sum(gsum, axis=1, keepdims=True), (per_exp, 128))
+            g = gcol[e]
             for n in range(0, HSUB, 2):
                 o = jnp.dot(hid[e], ring[slot, 0:ff, n * 128:(n + 2) * 128], preferred_element_type=F32)
                 for q in range(2):
@@ -474,6 +479,15 @@
         return carry
 
     lax.fori_loop(0, nh, half_step, 0)
+    for k in range(nc):
+        for n in range(13):
+            ag(k, n).wait_send()
+    for h in range(nh):
+        for b in range(n_blk):
+            d2d(h, b).wait_send()
+        for n in range(6):
+            if h < nh - 1 or n < 4:
+                link(h, n).wait_send()
     outs = []
     for h in range(nh):
         final(h)
@@ -481,14 +495,8 @@
                                     ysem.at[h])
         out.start()
         outs.append(out)
-    for k in range(nc):
-        for n in range(13):
-            ag(k, n).wait_send()
-    for h in range(nh):
-        for b in range(n_blk):
-            d2d(h, b).wait_send()
-        for n in range(6):
-            link(h, n).wait_send()
+    for n in (4, 5):
+        link(nh - 1, n).wait_send()
     for out in outs:
         out.wait()
 
@@ -519,6 +527,7 @@
             pltpu.VMEM((n_loc + 8, 256), jnp.int32),
             pltpu.VMEM((n_tok // 16, 128), jnp.int32),
             pltpu.VMEM((n_tok, 128), jnp.int32),
+            pltpu.VMEM((n_loc, per_exp, 128), F32),
             pltpu.VMEM((8 * (per_exp + 8), 128), F32),
             pltpu.VMEM((per_exp, kc), BF16),
             pltpu.VMEM((acc_rows // 8, 8, 128), F32),

time: 107 us -> 106 us (level)
    pallas_call x1, Pallas kernels: 105 us -> 104 us  [local_layer(): pl.pallas_call(functools.partial(moe_kernel, dims), out_shape=jax.ShapeDt...]
where the time goes in v4:
time: 106 us
  Pallas kernels  104 us (98%)
  local copies, waits for them, and re-layouts  2.47 us (2%)
    pallas_call x1, Pallas kernels, local_layer(): pl.pallas_call(functools.partial(moe_kernel, dims), out_shape=jax.ShapeDt...  104 us
    unnamed x1, local copies, waits for them, and re-layouts  2.47 us

profile of v4, /device:TPU:0, one launch (start us, length us, event | category | flops | bytes accessed | tf_op | source)
XLA Modules:
  0.0 106.0 jit_solution(17149949869404241017)
XLA Ops:
  0.0 103.6 %shard_map.64 = bf16[256,16,128]{2,1,0:T(8,128)(2,1)} custom-call(bf16[256,2048]{1,0:T(8,128)(2,1)} %x_hbm.1, s32[6,256]{1,0:T(8,128)} %bitcast.7, f32[6,256]{1,0:T(8,128)} %bitcast.8, bf16[8,2048,1408]{2,1,0:T(8,128)(2,1)} %w1_hbm.1, bf16[8,2048,1408]{2,1,0:T(8,128)(2,1)} %w3_hbm.1, bf16[8,1408,2048]{2,1,0:T(8,128)(2,1)} %w2_hbm.1), custom_call_target="tpu_custom_call" | custom-call | tf_op jit(solution)/shard_map/pallas_call | solution.py:559
  103.6 2.5 %copy.9 = bf16[32,8,16,128]{3,1,2,0:T(8,128)(2,1)} copy(bf16[32,8,16,128]{3,2,1,0:T(8,128)(2,1)} %bitcast.6) | data formatting | bytes 2097152

commit v5 on v4

--- a/solution.py
+++ b/solution.py
@@ -315,7 +315,7 @@
             proj_step(k, e)
             if k + 1 < nc:
                 if k > 0:
-                    @pl.when(e == 1)
+                    @pl.when(e == 0)
                     def _():
                         relay1(k + 1)
                         if k + 2 < nc:

time: 106 us -> 105 us (level)
  no operation moved by 1% of the time
where the time goes in v5:
time: 105 us
  Pallas kernels  103 us (98%)
  local copies, waits for them, and re-layouts  2.47 us (2%)
    pallas_call x1, Pallas kernels, local_layer(): pl.pallas_call(functools.partial(moe_kernel, dims), out_shape=jax.ShapeDt...  103 us
    unnamed x1, local copies, waits for them, and re-layouts  2.47 us

profile of v5, /device:TPU:0, one launch (start us, length us, event | category | flops | bytes accessed | tf_op | source)
XLA Modules:
  0.0 105.0 jit_solution(2148239738034799140)
XLA Ops:
  0.0 102.6 %shard_map.64 = bf16[256,16,128]{2,1,0:T(8,128)(2,1)} custom-call(bf16[256,2048]{1,0:T(8,128)(2,1)} %x_hbm.1, s32[6,256]{1,0:T(8,128)} %bitcast.7, f32[6,256]{1,0:T(8,128)} %bitcast.8, bf16[8,2048,1408]{2,1,0:T(8,128)(2,1)} %w1_hbm.1, bf16[8,2048,1408]{2,1,0:T(8,128)(2,1)} %w3_hbm.1, bf16[8,1408,2048]{2,1,0:T(8,128)(2,1)} %w2_hbm.1), custom_call_target="tpu_custom_call" | custom-call | tf_op jit(solution)/shard_map/pallas_call | solution.py:559
  102.6 2.5 %copy.9 = bf16[32,8,16,128]{3,1,2,0:T(8,128)(2,1)} copy(bf16[32,8,16,128]{3,2,1,0:T(8,128)(2,1)} %bitcast.6) | data formatting | bytes 2097152
